TPU v7x, 32 devices: a whole 2x2x4 slice. The times are simulated.
32 devices in a mesh: task: 4 (over z), mp: 8 (over y, x, core).
Axes of the slice: x: 2, y: 2, z: 4, core: 2. Of those that a mesh axis runs over, the one named last changes fastest.
Arguments:
- deter: float32 [1024, 4096], P('task', 'mp'), may hold values from -3 to 3
- draws: int32 [4, 32, 1024], P(None, None, 'task'), may hold values from 0 to 31
- actions: int32 [4, 1024], P(None, 'task'), may hold values from 0 to 17
- horizons: int32 [64], replicated, may hold values from 5 to 30, as said below
- offsets: int32 [4, 4], replicated, may hold values from 0 to 3, as said below
- embed_stoch: bfloat16 [1024, 1024], replicated, may hold values from -1 to 1
- embed_act: bfloat16 [18, 1024], replicated, may hold values from -6 to 6
- gru_weight: bfloat16 [5120, 3, 4096], P(None, None, 'mp'), may hold values from -0.078125 to 0.078125
- prior_weight: bfloat16 [4096, 1024], replicated, may hold values from -0.09375 to 0.09375
- logit_weight: bfloat16 [1024, 1024], replicated, may hold values from -0.75 to 0.75
- head_weight: bfloat16 [1024, 2], replicated, may hold values from -0.375 to 0.375
Outputs:
- log_prob: float32 [4, 1024], P(None, 'task')
- reward: float32 [4, 1024], P(None, 'task')
- continuation: float32 [4, 1024], P(None, 'task')
- final_deter: float32 [1024, 4096], P('task', 'mp')
Inputs may be any that keep to these rules, and one draw needn't show every extreme that they name: `horizons`: rows of task k are home rows k * (16) up to (k + 1) * 16 - 1. `offsets`: the 4 numbers of one row are distinct.
All inputs are finite; a program needn't handle non-finite values.
Results may differ from a plain program's by a relative error of at most 0.0045.
Values may be sent and summed in bfloat16 or wider, within the bound.
A program may use at most 128 MiB of HBM per device.

v0:
```python
import jax
import jax.numpy as jnp
from jax import lax
from jax.sharding import PartitionSpec as P

HID = 1024
GROUPS = 32
CLASSES = 32
ACTS = 18
TASKS = 64
BLK_DEV = 4
STEPS = 4
WSTART = 16


def layer_scale(column_sum, squares, entries):
    average = column_sum / entries
    return (average, lax.rsqrt(squares / entries - average * average + 1e-05))


def product(rows_in, weight):
    result = jnp.dot(rows_in, weight, preferred_element_type=jnp.float32)
    return result


def on_device(
    deter,
    draws,
    actions,
    horizons,
    offsets,
    embed_stoch,
    embed_act,
    gru_weight,
    prior_weight,
    logit_weight,
    head_weight,
):
    holders = lax.axis_size("task")
    device = lax.axis_index("task")
    shards = lax.axis_size("mp")
    shard_index = lax.axis_index("mp")
    rows_here = deter.shape[0]
    det_share = deter.shape[1]
    det_full = det_share * shards
    block_rows = rows_here // BLK_DEV
    per_task = rows_here * holders // TASKS
    hid_share = HID // shards
    places = jnp.arange(holders, dtype=jnp.int32)
    local_slot = jnp.arange(BLK_DEV, dtype=jnp.int32)
    within = jnp.arange(block_rows, dtype=jnp.int32)
    classes = jnp.arange(CLASSES, dtype=jnp.int32)
    action_ids = jnp.arange(ACTS, dtype=jnp.int32)
    task_ids = jnp.arange(TASKS, dtype=jnp.int32)
    gate_matrix = gru_weight.reshape(gru_weight.shape[0], 3 * det_share)
    carried = deter
    running = jnp.zeros((BLK_DEV,), jnp.int32)
    logp_list, reward_list, cont_list = ([], [], [])
    for moment in range(STEPS):
        offset_now = offsets[moment]
        target = (device + offset_now) % holders
        sending = (places[:, None] == target[None, :]).astype(jnp.float32)
        outgoing = jnp.einsum(
            "pj,jrc->prc",
            sending,
            carried.reshape(BLK_DEV, block_rows, det_share),
            precision=lax.Precision.HIGHEST,
        )
        arrived = lax.all_to_all(
            outgoing.reshape(holders * block_rows, det_share),
            "task",
            split_axis=0,
            concat_axis=0,
            tiled=True,
        )
        anchor = (device - offset_now) % holders
        taking = (anchor[:, None] == places[None, :]).astype(jnp.float32)
        carried = jnp.einsum(
            "jq,qrc->jrc",
            taking,
            arrived.reshape(holders, block_rows, det_share),
            precision=lax.Precision.HIGHEST,
        ).reshape(rows_here, det_share)
        running = (running + offset_now) % holders
        home_block = (device - running) % holders * BLK_DEV + local_slot
        home_rows = (home_block[:, None] * block_rows + within[None, :]).reshape(rows_here)
        row_task = home_rows // per_task
        horizon_rows = jnp.sum(
            jnp.where(row_task[:, None] == task_ids[None, :], horizons[None, :], 0), axis=1
        )
        living = (horizon_rows > WSTART + moment).astype(jnp.float32)
        chosen_hot = (jnp.transpose(draws[moment])[:, :, None] == classes).astype(jnp.float32)
        stoch_hot = chosen_hot.astype(jnp.bfloat16).reshape(rows_here, GROUPS * CLASSES)
        action_hot = (actions[moment][:, None] == action_ids[None, :]).astype(jnp.bfloat16)
        carried_low = carried.astype(jnp.bfloat16)
        stoch_cols = lax.dynamic_slice_in_dim(embed_stoch, shard_index * hid_share, hid_share, 1)
        act_cols = lax.dynamic_slice_in_dim(embed_act, shard_index * hid_share, hid_share, 1)
        embed_pre = jnp.dot(stoch_hot, stoch_cols, preferred_element_type=jnp.float32) + jnp.dot(
            action_hot, act_cols, preferred_element_type=jnp.float32
        )
        embed_sum, embed_square = lax.psum(
            (jnp.sum(embed_pre, axis=1), jnp.sum(embed_pre * embed_pre, axis=1)), "mp"
        )
        embed_avg, embed_inv = layer_scale(embed_sum, embed_square, HID)
        embed_cols = jax.nn.silu((embed_pre - embed_avg[:, None]) * embed_inv[:, None]).astype(
            jnp.bfloat16
        )
        embedded, gathered = (
            lax.all_gather(embed_cols, "mp", axis=1, tiled=True),
            lax.all_gather(carried_low, "mp", axis=1, tiled=True),
        )
        joined = jnp.concatenate([embedded, gathered], axis=1)
        gate_parts = product(joined, gate_matrix)
        part_sum = jnp.sum(gate_parts, axis=1)
        part_square = jnp.sum(gate_parts * gate_parts, axis=1)
        prior_cols = lax.dynamic_slice_in_dim(prior_weight, shard_index * hid_share, hid_share, 1)
        prior_pre = jnp.dot(gathered, prior_cols, preferred_element_type=jnp.float32)
        part_sum, part_square, prior_sum, prior_square = lax.psum(
            (
                part_sum,
                part_square,
                jnp.sum(prior_pre, axis=1),
                jnp.sum(prior_pre * prior_pre, axis=1),
            ),
            "mp",
        )
        prior_avg, prior_inv = layer_scale(prior_sum, prior_square, HID)
        hidden_cols = jax.nn.silu((prior_pre - prior_avg[:, None]) * prior_inv[:, None]).astype(
            jnp.bfloat16
        )
        hidden = lax.all_gather(hidden_cols, "mp", axis=1, tiled=True)
        gate_avg, gate_inv = layer_scale(part_sum, part_square, 3 * det_full)
        normed = ((gate_parts - gate_avg[:, None]) * gate_inv[:, None]).reshape(
            rows_here, 3, det_share
        )
        reset_gate = jax.nn.sigmoid(normed[:, 0])
        candidate = jnp.tanh(reset_gate * normed[:, 1])
        update = jax.nn.sigmoid(normed[:, 2] - 1.0)
        renewed = update * candidate + (1.0 - update) * carried
        raw_logits = product(hidden, logit_weight).reshape(rows_here, GROUPS, CLASSES)
        capped = 5.0 * jnp.tanh(raw_logits / 5.0)
        exponent = jnp.exp(capped)
        chances = 0.99 * exponent / jnp.sum(exponent, axis=-1, keepdims=True) + 0.01 / CLASSES
        log_prob = jnp.sum(jnp.log(jnp.sum(chances * chosen_hot, axis=-1)), axis=-1) * living
        head_out = jnp.dot(hidden, head_weight, preferred_element_type=jnp.float32)
        logp_list.append(log_prob)
        reward_list.append(head_out[:, 0] * living)
        cont_list.append(jax.nn.sigmoid(head_out[:, 1]) * living)
        carried = jnp.where(living[:, None] > 0, renewed, carried)
    return (jnp.stack(logp_list), jnp.stack(reward_list), jnp.stack(cont_list), carried)


def solution(mesh):
    in_specs = (
        P("task", "mp"),
        P(None, None, "task"),
        P(None, "task"),
        P(),
        P(),
        P(),
        P(),
        P(None, None, "mp"),
        P(),
        P(),
        P(),
    )
    out_specs = (P(None, "task"), P(None, "task"), P(None, "task"), P("task", "mp"))
    return jax.shard_map(
        on_device, mesh=mesh, in_specs=in_specs, out_specs=out_specs, check_vma=False
    )
```

profile of v0, /device:TPU:0, one launch (start us, length us, event | category | flops | bytes accessed | tf_op | source)
XLA Modules:
  0.0 457.1 jit_solution(11337123767255658716)
XLA Ops:
  7.2 1.5 fusion.193
  8.7 1.9 fusion.108
  11.6 6.3 %all-to-all-start = ((f32[4,64,512]{2,1,0:T(8,128)}), f32[4,64,512]{2,1,0:T(8,128)S(1)}, u32[]{:S(2)}, u32[]{:S(2)}) async-start(f32[4,64,512]{2,1,0:T(8,128)} %copy.115), calls=%async_computation | async-start | bytes 1048576 | tf_op jit(solution)/shard_map/all_to_all | solution.py:69
  18.7 13.8 %all-to-all-done = f32[4,64,512]{2,1,0:T(8,128)S(1)} async-done(((f32[4,64,512]{2,1,0:T(8,128)}), f32[4,64,512]{2,1,0:T(8,128)S(1)}, u32[]{:S(2)}, u32[]{:S(2)}) %all-to-all-start) | async-done | bytes 524320 | tf_op jit(solution)/shard_map/all_to_all | solution.py:69
  35.8 1.4 convert_convert_fusion
  37.5 1.3 fusion.229
  38.8 13.3 %all-reduce.4 = (f32[256]{0:T(256)S(1)}, f32[256]{0:T(256)S(1)}) all-reduce(f32[256]{0:T(256)S(1)} %get-tuple-element.39, f32[256]{0:T(256)S(1)} %get-tuple-element.38), channel_id=1, replica_groups=mesh['task'=4,'mp'=8] {'mp'}, use_global_device_ids=true, to_apply=%region_12.13 | all-reduce | flops 512 | bytes 4096 | tf_op jit(solution)/shard_map/psum | solution.py:101
  52.1 10.9 %all_gather.38 = bf16[256,1024]{0,1:T(8,128)(2,1)} all-gather(bf16[256,128]{0,1:T(8,128)(2,1)S(1)} %multiply_convert_fusion.6), channel_id=1, replica_groups=mesh['task'=4,'mp'=8] {'mp'}, dimensions={1}, use_global_device_ids=true | all-gather | bytes 589824 | tf_op jit(solution)/shard_map/all_gather | solution.py:109
  63.0 2.1 copy.120
  65.1 21.0 %copy.121 = bf16[5120,3,512]{0,2,1:T(8,128)(2,1)} copy(bf16[5120,3,512]{2,0,1:T(8,128)(2,1)} %param.18) | data formatting | bytes 31457280 | tf_op args[7]
  87.6 11.7 %fusion.221 = (f32[256]{0:T(256)S(1)}, f32[256]{0:T(256)S(1)}, f32[256,1536]{1,0:T(8,128)}) fusion(bf16[5120,1536]{0,1:T(8,128)(2,1)} %bitcast.208, bf16[256,4096]{1,0:T(8,128)(2,1)} %all-gather.5.cloned.1.call-done, bf16[256,1024]{1,0:T(8,128)(2,1)} %copy.120), kind=kOutput, calls=%fused_computation.439 | convolution fusion | flops 4032953856 | bytes 19924992 | tf_op jit(solution)/shard_map/dot_general | solution.py:22
  99.3 13.4 %all-reduce.3 = (f32[256]{0:T(256)S(1)}, f32[256]{0:T(256)S(1)}, f32[256]{0:T(256)S(1)}, f32[256]{0:T(256)S(1)}) all-reduce(f32[256]{0:T(256)S(1)} %get-tuple-element.23, f32[256]{0:T(256)S(1)} %get-tuple-element.22, f32[256]{0:T(256)S(1)} %get-tuple-element.37, f32[256]{0:T(256)S(1)} %get-tuple-element.36), channel_id=1, replica_groups=mesh['task'=4,'mp'=8] {'mp'}, use_global_device_ids=true, to_apply=%region_16.17 | all-reduce | flops 1024 | bytes 8192 | tf_op jit(solution)/shard_map/psum | solution.py:118
  112.7 2.8 subtract_multiply_fusion.3
  115.5 3.1 copy.122
  118.5 2.7 broadcast_subtract_fusion.2
  122.5 2.0 copy.123
  124.5 2.2 fusion.104
  126.9 16.4 %all_to_all.24 = f32[4,64,512]{2,1,0:T(8,128)S(1)} all-to-all(f32[4,64,512]{2,1,0:T(8,128)S(1)} %copy.127), channel_id=1, replica_groups=mesh['task'=4,'mp'=8] {'task'}, dimensions={0} | all-to-all | bytes 1048576 | tf_op jit(solution)/shard_map/all_to_all | solution.py:69
  147.5 10.7 %all_gather.41 = bf16[256,1024]{0,1:T(8,128)(2,1)S(1)} all-gather(bf16[256,128]{0,1:T(8,128)(2,1)S(1)} %multiply_convert_fusion.4), channel_id=1, replica_groups=mesh['task'=4,'mp'=8] {'mp'}, dimensions={1}, use_global_device_ids=true | all-gather | bytes 589824 | tf_op jit(solution)/shard_map/all_gather | solution.py:109
  159.2 12.7 %all-gather.7.cloned.1.call-done = bf16[256,4096]{1,0:T(8,128)(2,1)} async-done(((bf16[256,512]{1,0:T(8,128)(2,1)}), bf16[256,4096]{1,0:T(8,128)(2,1)}) %all-gather.7.cloned.1.call-update) | async-done | bytes 2097168 | tf_op jit(solution)/shard_map/all_gather | solution.py:110
  171.9 11.7 %fusion.220 = (f32[256]{0:T(256)S(1)}, f32[256]{0:T(256)S(1)}, f32[256,1536]{1,0:T(8,128)}) fusion(bf16[5120,1536]{0,1:T(8,128)(2,1)} %bitcast.209, bf16[256,4096]{1,0:T(8,128)(2,1)} %all-gather.7.cloned.1.call-done, bf16[256,1024]{1,0:T(8,128)(2,1)} %copy.132), kind=kOutput, calls=%fused_computation.438 | convolution fusion | flops 4032953856 | bytes 19924992 | tf_op jit(solution)/shard_map/dot_general | solution.py:22
  183.6 13.9 %all-reduce.2 = (f32[256]{0:T(256)S(1)}, f32[256]{0:T(256)S(1)}, f32[256]{0:T(256)}, f32[256]{0:T(256)}) all-reduce(f32[256]{0:T(256)S(1)} %get-tuple-element.21, f32[256]{0:T(256)S(1)} %get-tuple-element.20, f32[256]{0:T(256)S(1)} %get-tuple-element.35, f32[256]{0:T(256)S(1)} %get-tuple-element.34), channel_id=1, replica_groups=mesh['task'=4,'mp'=8] {'mp'}, use_global_device_ids=true, to_apply=%region_32.33 | all-reduce | flops 1024 | bytes 8192 | tf_op jit(solution)/shard_map/psum | solution.py:118
  197.4 2.8 subtract_multiply_fusion.2
  200.2 3.0 copy.133
  203.3 2.7 broadcast_subtract_fusion.1
  207.3 2.0 copy.134
  209.3 2.2 fusion.99
  211.7 17.6 %all_to_all.25 = f32[4,64,512]{2,1,0:T(8,128)S(1)} all-to-all(f32[4,64,512]{2,1,0:T(8,128)S(1)} %copy.138), channel_id=1, replica_groups=mesh['task'=4,'mp'=8] {'task'}, dimensions={0} | all-to-all | bytes 1048576 | tf_op jit(solution)/shard_map/all_to_all | solution.py:69
  231.5 1.8 fusion.222
  234.1 10.3 %all_gather.44 = bf16[256,1024]{0,1:T(8,128)(2,1)S(1)} all-gather(bf16[256,128]{0,1:T(8,128)(2,1)S(1)} %multiply_convert_fusion.2), channel_id=1, replica_groups=mesh['task'=4,'mp'=8] {'mp'}, dimensions={1}, use_global_device_ids=true | all-gather | bytes 589824 | tf_op jit(solution)/shard_map/all_gather | solution.py:109
  245.4 12.5 %all-gather.9.cloned.1.call-done = bf16[256,4096]{1,0:T(8,128)(2,1)} async-done(((bf16[256,512]{1,0:T(8,128)(2,1)}), bf16[256,4096]{1,0:T(8,128)(2,1)}) %all-gather.9.cloned.1.call-update) | async-done | bytes 2097168 | tf_op jit(solution)/shard_map/all_gather | solution.py:110
  257.9 11.7 %fusion.219 = (f32[256]{0:T(256)S(1)}, f32[256]{0:T(256)S(1)}, f32[256,1536]{1,0:T(8,128)}) fusion(bf16[5120,1536]{0,1:T(8,128)(2,1)} %bitcast.210, bf16[256,4096]{1,0:T(8,128)(2,1)} %all-gather.9.cloned.1.call-done, bf16[256,1024]{1,0:T(8,128)(2,1)} %copy.143), kind=kOutput, calls=%fused_computation.437 | convolution fusion | flops 4032953856 | bytes 19924992 | tf_op jit(solution)/shard_map/dot_general | solution.py:22
  269.6 14.1 %all-reduce.1 = (f32[256]{0:T(256)S(1)}, f32[256]{0:T(256)S(1)}, f32[256]{0:T(256)}, f32[256]{0:T(256)}) all-reduce(f32[256]{0:T(256)S(1)} %get-tuple-element.19, f32[256]{0:T(256)S(1)} %get-tuple-element.18, f32[256]{0:T(256)S(1)} %copy-done.22, f32[256]{0:T(256)S(1)} %get-tuple-element.24), channel_id=1, replica_groups=mesh['task'=4,'mp'=8] {'mp'}, use_global_device_ids=true, to_apply=%region_48.49 | all-reduce | flops 1024 | bytes 8192 | tf_op jit(solution)/shard_map/psum | solution.py:118
  283.7 2.8 subtract_multiply_fusion.1
  286.6 3.0 copy.144
  289.6 2.7 broadcast_subtract_fusion
  293.5 2.0 copy.145
  295.6 2.2 fusion.94
  297.9 17.6 %all_to_all.26 = f32[4,64,512]{2,1,0:T(8,128)S(1)} all-to-all(f32[4,64,512]{2,1,0:T(8,128)S(1)} %copy.149), channel_id=1, replica_groups=mesh['task'=4,'mp'=8] {'task'}, dimensions={0} | all-to-all | bytes 1048576 | tf_op jit(solution)/shard_map/all_to_all | solution.py:69
  318.0 2.8 fusion.223
  320.8 2.1 fusion.224
  323.0 10.4 %all_gather.47 = bf16[256,1024]{0,1:T(8,128)(2,1)S(1)} all-gather(bf16[256,128]{0,1:T(8,128)(2,1)S(1)} %multiply_convert_fusion), channel_id=1, replica_groups=mesh['task'=4,'mp'=8] {'mp'}, dimensions={1}, use_global_device_ids=true | all-gather | bytes 589824 | tf_op jit(solution)/shard_map/all_gather | solution.py:109
  334.4 3.0 fusion.225
  338.5 6.5 %all-gather.11.cloned.1.call-done = bf16[256,4096]{1,0:T(8,128)(2,1)} async-done(((bf16[256,512]{1,0:T(8,128)(2,1)}), bf16[256,4096]{1,0:T(8,128)(2,1)}) %all-gather.11.cloned.1.call-update) | async-done | bytes 2097168 | tf_op jit(solution)/shard_map/all_gather | solution.py:110
  345.0 2.7 fusion.226
  347.7 11.7 %fusion.218 = (f32[256]{0:T(256)S(1)}, f32[256]{0:T(256)S(1)}, f32[256,1536]{1,0:T(8,128)}) fusion(bf16[5120,1536]{0,1:T(8,128)(2,1)} %bitcast.211, bf16[256,4096]{1,0:T(8,128)(2,1)} %all-gather.11.cloned.1.call-done, bf16[256,1024]{1,0:T(8,128)(2,1)} %copy.153), kind=kOutput, calls=%fused_computation.436 | convolution fusion | flops 4032953856 | bytes 19924992 | tf_op jit(solution)/shard_map/dot_general | solution.py:22
  359.4 23.8 %all-reduce = (f32[256]{0:T(256)S(1)}, f32[256]{0:T(256)S(1)}, f32[256]{0:T(256)S(1)}, f32[256]{0:T(256)S(1)}, f32[256]{0:T(256)S(1)}, /*index=5*/f32[256]{0:T(2...) all-reduce(f32[256]{0:T(256)S(1)} %get-tuple-element.33, ...), channel_id=1, replica_groups=mesh['task'=4,'mp'=8] {'mp'}, use_global_device_ids=true, to_apply=%region_52.53 | all-reduce | flops 2560 | bytes 20480 | tf_op jit(solution)/shard_map/psum | solution.py:118
  383.2 9.8 %all_gather.43 = bf16[256,1024]{0,1:T(8,128)(2,1)S(1)} all-gather(bf16[256,128]{0,1:T(8,128)(2,1)S(1)} %multiply_convert_fusion.3), channel_id=1, replica_groups=mesh['task'=4,'mp'=8] {'mp'}, dimensions={1}, use_global_device_ids=true | all-gather | bytes 589824 | tf_op jit(solution)/shard_map/all_gather | solution.py:131
  393.1 8.9 %all_gather.46 = bf16[256,1024]{0,1:T(8,128)(2,1)S(1)} all-gather(bf16[256,128]{0,1:T(8,128)(2,1)S(1)} %multiply_convert_fusion.1), channel_id=1, replica_groups=mesh['task'=4,'mp'=8] {'mp'}, dimensions={1}, use_global_device_ids=true | all-gather | bytes 589824 | tf_op jit(solution)/shard_map/all_gather | solution.py:131
  402.4 1.9 fusion.34
  405.2 9.8 %all_gather.40 = bf16[256,1024]{0,1:T(8,128)(2,1)S(1)} all-gather(bf16[256,128]{0,1:T(8,128)(2,1)S(1)} %multiply_convert_fusion.5), channel_id=1, replica_groups=mesh['task'=4,'mp'=8] {'mp'}, dimensions={1}, use_global_device_ids=true | all-gather | bytes 589824 | tf_op jit(solution)/shard_map/all_gather | solution.py:131
  415.2 1.9 fusion.40
  417.2 8.9 %all_gather.37 = bf16[256,1024]{0,1:T(8,128)(2,1)S(1)} all-gather(bf16[256,128]{0,1:T(8,128)(2,1)S(1)} %multiply_convert_fusion.7), channel_id=1, replica_groups=mesh['task'=4,'mp'=8] {'mp'}, dimensions={1}, use_global_device_ids=true | all-gather | bytes 589824 | tf_op jit(solution)/shard_map/all_gather | solution.py:131
  426.2 1.9 fusion.43
  428.1 1.4 subtract_multiply_fusion
  429.5 3.0 copy.154
  432.5 2.5 copy.152
  435.0 1.9 fusion.234
  437.0 1.3 copy.141
  438.3 2.0 fusion.235
  440.3 1.3 copy.130
  441.6 2.0 fusion.236
  443.7 1.3 copy.118
  445.0 2.1 fusion.237
  (168 shorter events, 29.8 us)
Async XLA Ops:
  7.2 395.2 %copy-start = (bf16[1024,1024]{1,0:T(8,128)(2,1)S(1)}, bf16[1024,1024]{1,0:T(8,128)(2,1)}, u32[]{:S(2)}) copy-start(bf16[1024,1024]{1,0:T(8,128)(2,1)} %param.20) | copy-start | bytes 6291460
  7.2 10.8 %copy-start.19 = (s32[4,4]{1,0:T(4,128)S(1)}, s32[4,4]{1,0:T(4,128)}, u32[]{:S(2)}) copy-start(s32[4,4]{1,0:T(4,128)} %param.15) | copy-start | bytes 196
  10.6 24.2 %copy-start.32 = (s32[64]{0:T(128)S(1)}, s32[64]{0:T(128)}, u32[]{:S(2)}) copy-start(s32[64]{0:T(128)} %param.14) | copy-start | bytes 772
  10.6 25.1 %copy-start.17 = (s32[4,32,256]{2,1,0:T(8,128)S(1)}, s32[4,32,256]{2,1,0:T(8,128)}, u32[]{:S(2)}) copy-start(s32[4,32,256]{2,1,0:T(8,128)} %param.12) | copy-start | bytes 393220
  11.6 20.8 %all-to-all-start = ((f32[4,64,512]{2,1,0:T(8,128)}), f32[4,64,512]{2,1,0:T(8,128)S(1)}, u32[]{:S(2)}, u32[]{:S(2)}) async-start(f32[4,64,512]{2,1,0:T(8,128)} %copy.115), calls=%async_computation | async-start | bytes 1048576 | tf_op jit(solution)/shard_map/all_to_all | solution.py:69
  17.9 69.6 %all-gather.5.cloned.1.call-start = ((), (), s32[]{:S(2)}) async-start(), calls=%async_computation.4 | async-start | bytes 2359296 | tf_op jit(solution)/shard_map/all_gather | solution.py:110
  32.4 4.8 %copy-start.21 = (s32[4,256]{1,0:T(4,128)S(1)}, s32[4,256]{1,0:T(4,128)}, u32[]{:S(2)}) copy-start(s32[4,256]{1,0:T(4,128)} %param.13) | copy-start | bytes 12292
  32.4 4.8 %copy-start.20 = (bf16[18,1024]{1,0:T(8,128)(2,1)S(1)}, bf16[18,1024]{1,0:T(8,128)(2,1)}, u32[]{:S(2)}) copy-start(bf16[18,1024]{1,0:T(8,128)(2,1)} %param.17) | copy-start | bytes 110596
  34.1 137.8 %all-gather.7.cloned.1.call-start = ((), (), s32[]{:S(2)}) async-start(), calls=%async_computation.5 | async-start | bytes 2359296 | tf_op jit(solution)/shard_map/all_gather | solution.py:110
  35.8 3.0 copy-start.9
  35.8 3.0 copy-start.11
  35.8 3.0 copy-start.13
  35.8 3.0 copy-start.15
  126.7 19.4 %copy-start.5 = (bf16[256,1024]{0,1:T(8,128)(2,1)S(1)}, bf16[256,1024]{0,1:T(8,128)(2,1)}, u32[]{:S(2)}) copy-start(bf16[256,1024]{0,1:T(8,128)(2,1)} %get-tuple-element.93) | copy-start | bytes 1572868
  145.0 112.9 %all-gather.9.cloned.1.call-start = ((), (), s32[]{:S(2)}) async-start(), calls=%async_computation.6 | async-start | bytes 2359296 | tf_op jit(solution)/shard_map/all_gather | solution.py:110
  211.5 20.0 %copy-start.4 = (bf16[256,1024]{0,1:T(8,128)(2,1)S(1)}, bf16[256,1024]{0,1:T(8,128)(2,1)}, u32[]{:S(2)}) copy-start(bf16[256,1024]{0,1:T(8,128)(2,1)} %get-tuple-element.91) | copy-start | bytes 1572868
  231.0 114.0 %all-gather.11.cloned.1.call-start = ((), (), s32[]{:S(2)}) async-start(), calls=%async_computation.7 | async-start | bytes 2359296 | tf_op jit(solution)/shard_map/all_gather | solution.py:110
  245.4 24.2 %copy-start.22 = (f32[256]{0:T(256)S(1)}, f32[256]{0:T(256)}, u32[]{:S(2)}) copy-start(f32[256]{0:T(256)} %get-tuple-element.25) | copy-start | bytes 3076
  289.6 6.0 %copy-start.23 = (s32[4]{0:T(128)S(1)}, s32[4]{0:T(128)}, u32[]{:S(2)}) copy-start(s32[4]{0:T(128)} %get-tuple-element.114) | copy-start | bytes 52
  295.6 20.0 %copy-start.24 = (s32[4]{0:T(128)S(1)}, s32[4]{0:T(128)}, u32[]{:S(2)}) copy-start(s32[4]{0:T(128)} %get-tuple-element.107) | copy-start | bytes 52
  317.4 3.3 copy-start.6
  320.8 2.2 copy-start.30
  320.8 2.1 copy-start.31
  347.7 54.3 %copy-start.18 = (bf16[1024,2]{0,1:T(2,128)(2,1)S(1)}, bf16[1024,2]{0,1:T(2,128)(2,1)}, u32[]{:S(2)}) copy-start(bf16[1024,2]{0,1:T(2,128)(2,1)} %param.21) | copy-start | bytes 12292
  426.0 2.1 copy-start.8
  429.5 5.6 %copy-start.16 = (s32[256,32]{0,1:T(8,128)S(1)}, s32[256,32]{0,1:T(8,128)}, u32[]{:S(2)}) copy-start(s32[256,32]{0,1:T(8,128)} %copy-done.15) | copy-start | bytes 98308
  436.9 1.3 copy-start.14
  438.3 2.0 copy-start.2
  440.3 1.3 copy-start.12
  441.6 2.0 copy-start.3
  443.6 1.3 copy-start.10
  445.0 2.1 copy-start.1
  445.0 2.1 copy-start.7
  445.0 2.1 copy-start.29
  447.0 1.5 copy-start.26
  447.0 1.5 copy-start.28
  447.0 1.5 copy-start.27
  447.1 1.5 copy-start.25
Sparse Core Ops, SparseCore 0:
  34.2 28.5 all-gather.4
  145.2 26.6 all-gather.6
  231.1 26.7 all-gather.8
  317.5 27.4 all-gather.10
where the time goes:
time: 466 us; the launch traced here: 457 us
  blocking collectives  210 us (45%)
  matrix products  83.4 us (18%)
  local copies, waits for them, and re-layouts  61.5 us (13%)
  waiting for transfers between devices  45.6 us (10%)
  other arithmetic  35.8 us (8%)
  between operations  14.6 us (3%)
  starting transfers between devices  6.47 us (1%)
    psum x4, blocking collectives, on_device(): lax.psum((part_sum, part_square, jnp.sum(prior_pre, axis=1), jnp.sum(prio...  65 us
    dot_general x8, matrix products, product(): result = jnp.dot(rows_in, weight, preferred_element_type=jnp.float32)  53.3 us
    all_to_all x3, blocking collectives, on_device(): lax.all_to_all(outgoing.reshape(holders * block_rows, det_share), 'task',...  51.7 us
    all_gather x4, blocking collectives, on_device(): lax.all_gather(embed_cols, 'mp', axis=1, tiled=True)  42.3 us
    all_gather x4, blocking collectives, on_device(): hidden = lax.all_gather(hidden_cols, 'mp', axis=1, tiled=True)  37.4 us
    all_gather x4, waiting for transfers between devices, on_device(): lax.all_gather(carried_low, 'mp', axis=1, tiled=True)  31.8 us
    unnamed x68, local copies, waits for them, and re-layouts  22.1 us
    all_to_all x1, waiting for transfers between devices, on_device(): lax.all_to_all(outgoing.reshape(holders * block_rows, det_share), 'task',...  13.8 us
  transfers between devices with their start and end apart: 5, of which 4 were waited for; matrix products, arithmetic and copies ran while one was open for 10% of the time, Pallas kernels for 0%

commit v1 on v0

--- a/solution.py
+++ b/solution.py
@@ -107,7 +107,7 @@
         )
         embedded, gathered = (
             lax.all_gather(embed_cols, "mp", axis=1, tiled=True),
-            lax.all_gather(carried_low, "mp", axis=1, tiled=True),
+            jnp.concatenate(lax.all_gather(carried_low, "mp"), axis=1),
         )
         joined = jnp.concatenate([embedded, gathered], axis=1)
         gate_parts = product(joined, gate_matrix)

time: 466 us -> 480 us (1.030)
  local copies, waits for them, and re-layouts: 61.5 us -> 73 us
    all_gather x4, local copies, waits for them, and re-layouts: 5.1 us -> 15.8 us  [on_device(): lax.all_gather(carried_low, 'mp')]
    unnamed x68 -> x86, local copies, waits for them, and re-layouts: 22.1 us -> 22.1 us
where the time goes in v1:
time: 480 us; the launch traced here: 470 us
  blocking collectives  209 us (44%)
  matrix products  85.6 us (18%)
  local copies, waits for them, and re-layouts  73 us (15%)
  waiting for transfers between devices  45.1 us (9%)
  other arithmetic  36.6 us (8%)
  between operations  14.6 us (3%)
  starting transfers between devices  6.47 us (1%)
    psum x4, blocking collectives, on_device(): lax.psum((part_sum, part_square, jnp.sum(prior_pre, axis=1), jnp.sum(prio...  64.9 us
    dot_general x8, matrix products, product(): result = jnp.dot(rows_in, weight, preferred_element_type=jnp.float32)  52.8 us
    all_to_all x3, blocking collectives, on_device(): lax.all_to_all(outgoing.reshape(holders * block_rows, det_share), 'task',...  51 us
    all_gather x4, blocking collectives, on_device(): lax.all_gather(embed_cols, 'mp', axis=1, tiled=True)  41.9 us
    all_gather x4, blocking collectives, on_device(): hidden = lax.all_gather(hidden_cols, 'mp', axis=1, tiled=True)  37.8 us
    all_gather x4, waiting for transfers between devices, on_device(): lax.all_gather(carried_low, 'mp')  31.2 us
    unnamed x86, local copies, waits for them, and re-layouts  22.1 us
    all_gather x4, local copies, waits for them, and re-layouts, on_device(): lax.all_gather(carried_low, 'mp')  15.8 us
  transfers between devices with their start and end apart: 5, of which 4 were waited for; matrix products, arithmetic and copies ran while one was open for 10% of the time, Pallas kernels for 0%

profile of v1, /device:TPU:0, one launch (start us, length us, event | category | flops | bytes accessed | tf_op | source)
XLA Modules:
  0.0 470.2 jit_solution(5162425296502098539)
XLA Ops:
  7.2 1.4 fusion.193
  8.6 1.9 fusion.108
  11.5 6.3 %all-to-all-start = ((f32[4,64,512]{2,1,0:T(8,128)}), f32[4,64,512]{2,1,0:T(8,128)S(1)}, u32[]{:S(2)}, u32[]{:S(2)}) async-start(f32[4,64,512]{2,1,0:T(8,128)} %copy.117), calls=%async_computation | async-start | bytes 1048576 | tf_op jit(solution)/shard_map/all_to_all | solution.py:69
  18.6 13.8 %all-to-all-done = f32[4,64,512]{2,1,0:T(8,128)S(1)} async-done(((f32[4,64,512]{2,1,0:T(8,128)}), f32[4,64,512]{2,1,0:T(8,128)S(1)}, u32[]{:S(2)}, u32[]{:S(2)}) %all-to-all-start) | async-done | bytes 524320 | tf_op jit(solution)/shard_map/all_to_all | solution.py:69
  36.2 20.9 %copy.123 = bf16[5120,3,512]{0,2,1:T(8,128)(2,1)} copy(bf16[5120,3,512]{2,0,1:T(8,128)(2,1)} %param.18) | data formatting | bytes 31457280 | tf_op args[7]
  57.1 1.4 convert_convert_fusion
  60.7 13.2 %all-reduce.4 = (f32[256]{0:T(256)S(1)}, f32[256]{0:T(256)S(1)}) all-reduce(f32[256]{0:T(256)S(1)} %get-tuple-element.39, f32[256]{0:T(256)S(1)} %get-tuple-element.38), channel_id=1, replica_groups=mesh['task'=4,'mp'=8] {'mp'}, use_global_device_ids=true, to_apply=%region_12.13 | all-reduce | flops 512 | bytes 4096 | tf_op jit(solution)/shard_map/psum | solution.py:101
  74.0 9.9 %all_gather.42 = bf16[256,1024]{0,1:T(8,128)(2,1)} all-gather(bf16[256,128]{0,1:T(8,128)(2,1)S(1)} %multiply_convert_fusion.6), channel_id=1, replica_groups=mesh['task'=4,'mp'=8] {'mp'}, dimensions={1}, use_global_device_ids=true | all-gather | bytes 589824 | tf_op jit(solution)/shard_map/all_gather | solution.py:109
  86.2 4.0 copy.120
  90.2 11.6 %fusion.221 = (f32[256]{0:T(256)S(1)}, f32[256]{0:T(256)S(1)}, f32[256,1536]{1,0:T(8,128)}) fusion(bf16[5120,1536]{0,1:T(8,128)(2,1)} %bitcast.222, bf16[256,4096]{0,1:T(8,128)(2,1)} %bitcast.236, bf16[256,1024]{0,1:T(8,128)(2,1)S(1)} %copy-done.11), kind=kOutput, calls=%fused_computation.438 | convolution fusion | flops 4032953856 | bytes 19924992 | tf_op jit(solution)/shard_map/dot_general | solution.py:22
  101.8 13.4 %all-reduce.3 = (f32[256]{0:T(256)S(1)}, f32[256]{0:T(256)S(1)}, f32[256]{0:T(256)S(1)}, f32[256]{0:T(256)S(1)}) all-reduce(f32[256]{0:T(256)S(1)} %get-tuple-element.23, f32[256]{0:T(256)S(1)} %get-tuple-element.22, f32[256]{0:T(256)S(1)} %get-tuple-element.37, f32[256]{0:T(256)S(1)} %get-tuple-element.36), channel_id=1, replica_groups=mesh['task'=4,'mp'=8] {'mp'}, use_global_device_ids=true, to_apply=%region_16.17 | all-reduce | flops 1024 | bytes 8192 | tf_op jit(solution)/shard_map/psum | solution.py:118
  115.7 2.8 subtract_multiply_fusion.3
  118.5 3.1 copy.124
  121.5 2.7 broadcast_subtract_fusion.2
  125.5 2.1 copy.125
  127.5 2.2 fusion.104
  129.9 15.8 %all_to_all.24 = f32[4,64,512]{2,1,0:T(8,128)S(1)} all-to-all(f32[4,64,512]{2,1,0:T(8,128)S(1)} %copy.129), channel_id=1, replica_groups=mesh['task'=4,'mp'=8] {'task'}, dimensions={0} | all-to-all | bytes 1048576 | tf_op jit(solution)/shard_map/all_to_all | solution.py:69
  149.2 1.8 fusion.227
  151.8 10.6 %all_gather.45 = bf16[256,1024]{0,1:T(8,128)(2,1)S(1)} all-gather(bf16[256,128]{0,1:T(8,128)(2,1)S(1)} %multiply_convert_fusion.4), channel_id=1, replica_groups=mesh['task'=4,'mp'=8] {'mp'}, dimensions={1}, use_global_device_ids=true | all-gather | bytes 589824 | tf_op jit(solution)/shard_map/all_gather | solution.py:109
  162.4 12.3 %all-gather.7.cloned.1.call-done = bf16[8,256,512]{2,1,0:T(8,128)(2,1)} async-done(((bf16[1,256,512]{2,1,0:T(8,128)(2,1)}), bf16[8,256,512]{2,1,0:T(8,128)(2,1)}) %all-gather.7.cloned.1.call-update) | async-done | bytes 2097168 | tf_op jit(solution)/shard_map/all_gather | solution.py:110
  174.6 3.9 copy.132
  178.5 11.5 %fusion.220 = (f32[256]{0:T(256)S(1)}, f32[256]{0:T(256)S(1)}, f32[256,1536]{1,0:T(8,128)}) fusion(bf16[5120,1536]{0,1:T(8,128)(2,1)} %bitcast.223, bf16[256,4096]{0,1:T(8,128)(2,1)} %bitcast.238, bf16[256,1024]{0,1:T(8,128)(2,1)S(1)} %all_gather.45), kind=kOutput, calls=%fused_computation.437 | convolution fusion | flops 4032953856 | bytes 19924992 | tf_op jit(solution)/shard_map/dot_general | solution.py:22
  190.1 13.9 %all-reduce.2 = (f32[256]{0:T(256)S(1)}, f32[256]{0:T(256)S(1)}, f32[256]{0:T(256)}, f32[256]{0:T(256)}) all-reduce(f32[256]{0:T(256)S(1)} %get-tuple-element.21, f32[256]{0:T(256)S(1)} %get-tuple-element.20, f32[256]{0:T(256)S(1)} %copy-done.19, f32[256]{0:T(256)S(1)} %copy-done.18), channel_id=1, replica_groups=mesh['task'=4,'mp'=8] {'mp'}, use_global_device_ids=true, to_apply=%region_32.33 | all-reduce | flops 1024 | bytes 8192 | tf_op jit(solution)/shard_map/psum | solution.py:118
  204.0 2.8 subtract_multiply_fusion.2
  206.8 3.0 copy.135
  209.8 2.7 broadcast_subtract_fusion.1
  213.8 2.0 copy.136
  215.8 2.2 fusion.99
  218.2 17.6 %all_to_all.25 = f32[4,64,512]{2,1,0:T(8,128)S(1)} all-to-all(f32[4,64,512]{2,1,0:T(8,128)S(1)} %copy.140), channel_id=1, replica_groups=mesh['task'=4,'mp'=8] {'task'}, dimensions={0} | all-to-all | bytes 1048576 | tf_op jit(solution)/shard_map/all_to_all | solution.py:69
  240.8 10.4 %all_gather.48 = bf16[256,1024]{0,1:T(8,128)(2,1)S(1)} all-gather(bf16[256,128]{0,1:T(8,128)(2,1)S(1)} %multiply_convert_fusion.2), channel_id=1, replica_groups=mesh['task'=4,'mp'=8] {'mp'}, dimensions={1}, use_global_device_ids=true | all-gather | bytes 589824 | tf_op jit(solution)/shard_map/all_gather | solution.py:109
  251.2 13.1 %all-gather.9.cloned.1.call-done = bf16[8,256,512]{2,1,0:T(8,128)(2,1)} async-done(((bf16[1,256,512]{2,1,0:T(8,128)(2,1)}), bf16[8,256,512]{2,1,0:T(8,128)(2,1)}) %all-gather.9.cloned.1.call-update) | async-done | bytes 2097168 | tf_op jit(solution)/shard_map/all_gather | solution.py:110
  264.3 3.9 copy.143
  268.2 11.5 %fusion.219 = (f32[256]{0:T(256)S(1)}, f32[256]{0:T(256)S(1)}, f32[256,1536]{1,0:T(8,128)}) fusion(bf16[5120,1536]{0,1:T(8,128)(2,1)} %bitcast.224, bf16[256,4096]{0,1:T(8,128)(2,1)} %bitcast.240, bf16[256,1024]{0,1:T(8,128)(2,1)S(1)} %all_gather.48), kind=kOutput, calls=%fused_computation.436 | convolution fusion | flops 4032953856 | bytes 19924992 | tf_op jit(solution)/shard_map/dot_general | solution.py:22
  279.8 14.0 %all-reduce.1 = (f32[256]{0:T(256)S(1)}, f32[256]{0:T(256)S(1)}, f32[256]{0:T(256)}, f32[256]{0:T(256)}) all-reduce(f32[256]{0:T(256)S(1)} %get-tuple-element.19, f32[256]{0:T(256)S(1)} %get-tuple-element.18, f32[256]{0:T(256)S(1)} %get-tuple-element.25, f32[256]{0:T(256)S(1)} %get-tuple-element.24), channel_id=1, replica_groups=mesh['task'=4,'mp'=8] {'mp'}, use_global_device_ids=true, to_apply=%region_48.49 | all-reduce | flops 1024 | bytes 8192 | tf_op jit(solution)/shard_map/psum | solution.py:118
  293.8 2.8 subtract_multiply_fusion.1
  296.7 3.0 copy.146
  299.7 2.7 broadcast_subtract_fusion
  303.6 2.0 copy.147
  305.7 2.2 fusion.94
  308.1 17.6 %all_to_all.26 = f32[4,64,512]{2,1,0:T(8,128)S(1)} all-to-all(f32[4,64,512]{2,1,0:T(8,128)S(1)} %copy.151), channel_id=1, replica_groups=mesh['task'=4,'mp'=8] {'task'}, dimensions={0} | all-to-all | bytes 1048576 | tf_op jit(solution)/shard_map/all_to_all | solution.py:69
  328.0 2.5 fusion.223
  330.5 3.2 fusion.224
  333.7 11.0 %all_gather.51 = bf16[256,1024]{0,1:T(8,128)(2,1)} all-gather(bf16[256,128]{0,1:T(8,128)(2,1)S(1)} %multiply_convert_fusion), channel_id=1, replica_groups=mesh['task'=4,'mp'=8] {'mp'}, dimensions={1}, use_global_device_ids=true | all-gather | bytes 589824 | tf_op jit(solution)/shard_map/all_gather | solution.py:109
  344.7 2.4 fusion.225
  348.2 5.9 %all-gather.11.cloned.1.call-done = bf16[8,256,512]{2,1,0:T(8,128)(2,1)} async-done(((bf16[1,256,512]{2,1,0:T(8,128)(2,1)}), bf16[8,256,512]{2,1,0:T(8,128)(2,1)}) %all-gather.11.cloned.1.call-update) | async-done | bytes 2097168 | tf_op jit(solution)/shard_map/all_gather | solution.py:110
  354.1 3.9 copy.154
  358.0 2.5 fusion.226
  360.6 11.6 %fusion.218 = (f32[256]{0:T(256)S(1)}, f32[256]{0:T(256)S(1)}, f32[256,1536]{1,0:T(8,128)}) fusion(bf16[5120,1536]{0,1:T(8,128)(2,1)} %bitcast.225, bf16[256,4096]{0,1:T(8,128)(2,1)} %bitcast.243, bf16[256,1024]{0,1:T(8,128)(2,1)S(1)} %copy-done.10), kind=kOutput, calls=%fused_computation.435 | convolution fusion | flops 4032953856 | bytes 19924992 | tf_op jit(solution)/shard_map/dot_general | solution.py:22
  372.2 23.6 %all-reduce = (f32[256]{0:T(256)S(1)}, f32[256]{0:T(256)S(1)}, f32[256]{0:T(256)S(1)}, f32[256]{0:T(256)S(1)}, f32[256]{0:T(256)}, /*index=5*/f32[256]{0:T(256)}...) all-reduce(f32[256]{0:T(256)S(1)} %get-tuple-element.33, ...), channel_id=1, replica_groups=mesh['task'=4,'mp'=8] {'mp'}, use_global_device_ids=true, to_apply=%region_52.53 | all-reduce | flops 2560 | bytes 20480 | tf_op jit(solution)/shard_map/psum | solution.py:118
  395.9 10.4 %all_gather.47 = bf16[256,1024]{0,1:T(8,128)(2,1)S(1)} all-gather(bf16[256,128]{0,1:T(8,128)(2,1)S(1)} %multiply_convert_fusion.3), channel_id=1, replica_groups=mesh['task'=4,'mp'=8] {'mp'}, dimensions={1}, use_global_device_ids=true | all-gather | bytes 589824 | tf_op jit(solution)/shard_map/all_gather | solution.py:131
  406.4 8.7 %all_gather.50 = bf16[256,1024]{0,1:T(8,128)(2,1)S(1)} all-gather(bf16[256,128]{0,1:T(8,128)(2,1)S(1)} %multiply_convert_fusion.1), channel_id=1, replica_groups=mesh['task'=4,'mp'=8] {'mp'}, dimensions={1}, use_global_device_ids=true | all-gather | bytes 589824 | tf_op jit(solution)/shard_map/all_gather | solution.py:131
  415.5 1.9 fusion.34
  418.4 10.0 %all_gather.44 = bf16[256,1024]{0,1:T(8,128)(2,1)S(1)} all-gather(bf16[256,128]{0,1:T(8,128)(2,1)S(1)} %multiply_convert_fusion.5), channel_id=1, replica_groups=mesh['task'=4,'mp'=8] {'mp'}, dimensions={1}, use_global_device_ids=true | all-gather | bytes 589824 | tf_op jit(solution)/shard_map/all_gather | solution.py:131
  428.6 1.9 fusion.40
  430.5 8.7 %all_gather.41 = bf16[256,1024]{0,1:T(8,128)(2,1)S(1)} all-gather(bf16[256,128]{0,1:T(8,128)(2,1)S(1)} %multiply_convert_fusion.7), channel_id=1, replica_groups=mesh['task'=4,'mp'=8] {'mp'}, dimensions={1}, use_global_device_ids=true | all-gather | bytes 589824 | tf_op jit(solution)/shard_map/all_gather | solution.py:131
  439.4 1.9 fusion.43
  441.2 1.4 subtract_multiply_fusion
  442.6 3.0 copy.156
  445.7 2.5 copy.155
  448.2 1.9 fusion.235
  450.1 1.3 copy.144
  451.4 2.0 fusion.236
  454.7 2.0 fusion.237
  458.1 2.0 fusion.238
  (186 shorter events, 35.2 us)
Async XLA Ops:
  7.2 408.3 %copy-start = (bf16[1024,1024]{1,0:T(8,128)(2,1)S(1)}, bf16[1024,1024]{1,0:T(8,128)(2,1)}, u32[]{:S(2)}) copy-start(bf16[1024,1024]{1,0:T(8,128)(2,1)} %param.20) | copy-start | bytes 6291460
  7.2 10.7 %copy-start.15 = (s32[4,4]{1,0:T(4,128)S(1)}, s32[4,4]{1,0:T(4,128)}, u32[]{:S(2)}) copy-start(s32[4,4]{1,0:T(4,128)} %param.15) | copy-start | bytes 196
  10.5 24.1 %copy-start.40 = (s32[64]{0:T(128)S(1)}, s32[64]{0:T(128)}, u32[]{:S(2)}) copy-start(s32[64]{0:T(128)} %param.14) | copy-start | bytes 772
  11.5 20.8 %all-to-all-start = ((f32[4,64,512]{2,1,0:T(8,128)}), f32[4,64,512]{2,1,0:T(8,128)S(1)}, u32[]{:S(2)}, u32[]{:S(2)}) async-start(f32[4,64,512]{2,1,0:T(8,128)} %copy.117), calls=%async_computation | async-start | bytes 1048576 | tf_op jit(solution)/shard_map/all_to_all | solution.py:69
  17.9 68.3 %all-gather.5.cloned.1.call-start = ((), (), s32[]{:S(2)}) async-start(), calls=%async_computation.4 | async-start | bytes 2359296 | tf_op jit(solution)/shard_map/all_gather | solution.py:110
  34.0 140.6 %all-gather.7.cloned.1.call-start = ((), (), s32[]{:S(2)}) async-start(), calls=%async_computation.5 | async-start | bytes 2359296 | tf_op jit(solution)/shard_map/all_gather | solution.py:110
  36.2 20.9 %copy-start.13 = (s32[4,32,256]{2,1,0:T(8,128)S(1)}, s32[4,32,256]{2,1,0:T(8,128)}, u32[]{:S(2)}) copy-start(s32[4,32,256]{2,1,0:T(8,128)} %param.12) | copy-start | bytes 393220
  57.1 1.4 copy-start.17
  86.2 4.0 copy-start.11
  129.7 19.4 %copy-start.5 = (bf16[256,1024]{0,1:T(8,128)(2,1)S(1)}, bf16[256,1024]{0,1:T(8,128)(2,1)}, u32[]{:S(2)}) copy-start(bf16[256,1024]{0,1:T(8,128)(2,1)} %get-tuple-element.93) | copy-start | bytes 1572868
  147.4 116.9 %all-gather.9.cloned.1.call-start = ((), (), s32[]{:S(2)}) async-start(), calls=%async_computation.6 | async-start | bytes 2359296 | tf_op jit(solution)/shard_map/all_gather | solution.py:110
  178.5 11.6 %copy-start.18 = (f32[256]{0:T(256)S(1)}, f32[256]{0:T(256)}, u32[]{:S(2)}) copy-start(f32[256]{0:T(256)} %get-tuple-element.34) | copy-start | bytes 3076
  178.5 11.6 %copy-start.19 = (f32[256]{0:T(256)S(1)}, f32[256]{0:T(256)}, u32[]{:S(2)}) copy-start(f32[256]{0:T(256)} %get-tuple-element.35) | copy-start | bytes 3076
  209.8 6.0 %copy-start.21 = (s32[4]{0:T(128)S(1)}, s32[4]{0:T(128)}, u32[]{:S(2)}) copy-start(s32[4]{0:T(128)} %get-tuple-element.116) | copy-start | bytes 52
  215.8 20.1 %copy-start.23 = (s32[4]{0:T(128)S(1)}, s32[4]{0:T(128)}, u32[]{:S(2)}) copy-start(s32[4]{0:T(128)} %get-tuple-element.113) | copy-start | bytes 52
  218.0 19.6 %copy-start.41 = (pred[256]{0:T(512)(128)(4,1)S(1)}, pred[256]{0:T(512)(128)(4,1)}, u32[]{:S(2)}) copy-start(pred[256]{0:T(512)(128)(4,1)} %get-tuple-element.70) | copy-start | bytes 772
  218.0 20.8 %copy-start.4 = (bf16[256,1024]{0,1:T(8,128)(2,1)S(1)}, bf16[256,1024]{0,1:T(8,128)(2,1)}, u32[]{:S(2)}) copy-start(bf16[256,1024]{0,1:T(8,128)(2,1)} %get-tuple-element.91) | copy-start | bytes 1572868
  237.6 116.5 %all-gather.11.cloned.1.call-start = ((), (), s32[]{:S(2)}) async-start(), calls=%async_computation.7 | async-start | bytes 2359296 | tf_op jit(solution)/shard_map/all_gather | solution.py:110
  299.7 6.0 %copy-start.20 = (s32[4]{0:T(128)S(1)}, s32[4]{0:T(128)}, u32[]{:S(2)}) copy-start(s32[4]{0:T(128)} %get-tuple-element.114) | copy-start | bytes 52
  305.7 20.0 %copy-start.22 = (s32[4]{0:T(128)S(1)}, s32[4]{0:T(128)}, u32[]{:S(2)}) copy-start(s32[4]{0:T(128)} %get-tuple-element.107) | copy-start | bytes 52
  307.9 19.5 %copy-start.16 = (s32[256]{0:T(256)S(1)}, s32[256]{0:T(256)}, u32[]{:S(2)}) copy-start(s32[256]{0:T(256)} %get-tuple-element.40) | copy-start | bytes 3076
  327.4 3.1 copy-start.6
  330.5 3.2 copy-start.34
  330.5 3.2 copy-start.35
  330.5 14.2 %copy-start.7 = (bf16[8,256,512]{1,2,0:T(8,128)(2,1)S(1)}, bf16[8,256,512]{1,2,0:T(8,128)(2,1)}, u32[]{:S(2)}) copy-start(bf16[8,256,512]{1,2,0:T(8,128)(2,1)} %copy.143) | copy-start | bytes 6291460
  358.0 2.5 copy-start.10
  360.5 11.6 %copy-start.28 = (f32[256]{0:T(256)S(1)}, f32[256]{0:T(256)}, u32[]{:S(2)}) copy-start(f32[256]{0:T(256)} %get-tuple-element.28) | copy-start | bytes 3076
  360.5 11.6 %copy-start.29 = (f32[256]{0:T(256)S(1)}, f32[256]{0:T(256)}, u32[]{:S(2)}) copy-start(f32[256]{0:T(256)} %get-tuple-element.29) | copy-start | bytes 3076
  360.5 11.6 %copy-start.30 = (f32[256]{0:T(256)S(1)}, f32[256]{0:T(256)}, u32[]{:S(2)}) copy-start(f32[256]{0:T(256)} %get-tuple-element.30) | copy-start | bytes 3076
  360.6 11.6 %copy-start.31 = (f32[256]{0:T(256)S(1)}, f32[256]{0:T(256)}, u32[]{:S(2)}) copy-start(f32[256]{0:T(256)} %get-tuple-element.31) | copy-start | bytes 3076
  360.6 54.5 %copy-start.14 = (bf16[1024,2]{0,1:T(2,128)(2,1)S(1)}, bf16[1024,2]{0,1:T(2,128)(2,1)}, u32[]{:S(2)}) copy-start(bf16[1024,2]{0,1:T(2,128)(2,1)} %param.21) | copy-start | bytes 12292
  417.4 0.9 copy-start.38
  417.4 0.9 copy-start.39
  417.4 0.9 copy-start.12
  428.4 2.0 copy-start.36
  428.4 2.0 copy-start.37
  439.2 2.1 copy-start.32
  439.2 2.1 copy-start.33
  439.2 2.1 copy-start.9
  451.4 2.0 copy-start.2
  454.7 2.0 copy-start.3
  458.1 2.1 copy-start.1
  458.1 2.1 copy-start.8
  458.1 2.1 copy-start.27
  460.1 1.5 copy-start.26
  460.1 1.5 copy-start.25
  460.2 1.5 copy-start.24
Sparse Core Ops, SparseCore 0:
  34.2 26.8 all-gather.4
  147.5 27.0 all-gather.6
  237.7 26.5 all-gather.8
  327.5 26.5 all-gather.10
